TPU v7x, 32 devices: a whole 2x2x4 slice. The times are simulated.
32 devices in a mesh: blk: 8 (over z, x), lay: 4 (over y, core).
Axes of the slice: x: 2, y: 2, z: 4, core: 2. Of those that a mesh axis runs over, the one named last changes fastest.
Arguments:
- three_centre: bfloat16 [512, 512, 512], P('blk', 'lay'), may hold values from -224 to 224, as said below
- metric: bfloat16 [512, 64], P('blk'), may hold values from -2 to 6
- tile_pattern: int32 [512, 16, 16], P('blk'), may hold values from 0 to 1, as said below
- density: bfloat16 [512, 512], P('lay'), may hold values from -0.00048828125 to 0.00048828125
- dens_pattern: int32 [16, 16], replicated, may hold values 0 or 1
Outputs:
- exchange: float32 [512, 512], P('lay')
Inputs may be any that keep to these rules, and one draw needn't show every extreme that they name: three_centre(P, mu, lambda) equals three_centre(P, lambda, mu). `tile_pattern`: symmetric in its last two dimensions; diagonal tiles are 1; the share of ones is drawn per group of 64 consecutive functions.
All inputs are finite; a program needn't handle non-finite values.
Results may differ from a plain program's by a relative error of at most 0.0043.
Values may be sent and summed in bfloat16 or wider, within the bound.
No kernel may reach another device: no remote copies, remote signals or barrier semaphores. Data moves between devices by JAX's collectives and lax.ppermute only.
A program may use at most 128 MiB of HBM per device.

v0:
```python
import jax
import jax.numpy as jnp
from jax import lax
from jax.sharding import PartitionSpec as P

TILE = 32


def density_adder(left_side, dens_pattern, segment):
    count = segment.shape[0]
    block_ids = jnp.arange(count, dtype=jnp.int32) // TILE
    row_pattern = jnp.take(dens_pattern, block_ids, axis=0)
    dens_mask = jnp.repeat(row_pattern, TILE, axis=1)
    kept = jnp.where(dens_mask > 0, segment, jnp.zeros_like(segment))
    return jnp.dot(left_side, kept, preferred_element_type=jnp.float32)


def per_device(three_centre, metric, tile_pattern, density, dens_pattern):
    group_size = three_centre.shape[0]
    row_count = three_centre.shape[1]
    ao_width = three_centre.shape[2]
    layers = lax.axis_size("lay")
    row_start = lax.axis_index("lay") * row_count
    row_blocks = (row_start + jnp.arange(row_count, dtype=jnp.int32)) // TILE
    pattern_rows = jnp.take(tile_pattern, row_blocks, axis=1)
    tile_mask = jnp.repeat(pattern_rows, TILE, axis=2)
    masked = jnp.where(tile_mask > 0, three_centre, jnp.zeros_like(three_centre))
    coeffs = jnp.einsum("pq,qmn->pmn", metric, masked, preferred_element_type=jnp.float32).astype(
        jnp.bfloat16
    )
    left_side = coeffs.reshape(group_size * row_count, ao_width)
    inter = density_adder(
        left_side, dens_pattern, lax.all_gather(density, "lay", axis=0, tiled=True)
    )
    column_count = ao_width // layers
    inter = inter.astype(jnp.bfloat16).reshape(group_size, row_count, layers, column_count)
    outgoing = jnp.transpose(inter, (2, 1, 0, 3)).reshape(
        layers, row_count, group_size * column_count
    )
    moved = lax.all_to_all(outgoing, "lay", split_axis=0, concat_axis=1, tiled=True)
    moved = moved.reshape(ao_width, group_size * column_count)
    partial_value = jnp.dot(
        moved, coeffs.reshape(group_size * row_count, ao_width), preferred_element_type=jnp.float32
    )
    row_sums = lax.psum_scatter(partial_value, "lay", scatter_dimension=0, tiled=True)
    return lax.psum(row_sums, "blk")


def solution(mesh):
    return jax.shard_map(
        per_device,
        mesh=mesh,
        in_specs=(P("blk", "lay", None), P("blk", None), P("blk", None, None), P("lay", None), P()),
        out_specs=P("lay", None),
        check_vma=False,
    )
```

profile of v0, /device:TPU:0, one launch (start us, length us, event | category | flops | bytes accessed | tf_op | source)
XLA Modules:
  0.0 340.7 jit_solution(9691291641924943559)
XLA Ops:
  6.5 0.0 copy-start
  6.5 0.0 reduce-scatter.2.cloned.1.call-start
  6.6 1.0 copy.28
  7.7 1.7 gather_fusion.1
  9.4 0.1 copy.27
  9.5 8.7 %all_gather.3 = bf16[512,512]{0,1:T(8,128)(2,1)S(1)} all-gather(bf16[128,512]{0,1:T(8,128)(2,1)S(1)} %copy.28), channel_id=1, replica_groups=mesh['blk'=8,'lay'=4] {'lay'}, dimensions={0}, use_global_device_ids=true | all-gather | bytes 655360 | tf_op jit(solution)/shard_map/all_gather | solution.py:33
  18.2 0.0 copy-done
  18.2 0.8 gather_fusion
  18.9 0.3 fusion
  19.2 0.7 copy.23
  19.9 11.9 %copy.24 = bf16[64,128,512]{1,2,0:T(8,128)(2,1)} copy(bf16[64,128,512]{2,1,0:T(8,128)(2,1)} %param.5) | data formatting | bytes 16777216 | tf_op args[0]
  31.9 7.5 %bitcast_select_fusion = bf16[64,128,512]{1,2,0:T(8,128)(2,1)} fusion(bf16[64,128,512]{1,2,0:T(8,128)(2,1)} %copy.24, pred[64,128,16]{1,2,0:T(8,128)(4,1)S(1)} %copy.23), kind=kLoop, calls=%fused_computation.2 | loop fusion | flops 4194304 | bytes 16908288 | tf_op jit(solution)/shard_map/jit(_where)/select_n | solution.py:27
  39.4 0.0 copy-start.2
  39.4 12.6 %copy.25 = bf16[64,128,512]{2,0,1:T(8,128)(2,1)} copy(bf16[64,128,512]{1,2,0:T(8,128)(2,1)} %bitcast_select_fusion) | data formatting | bytes 16777216 | tf_op jit(solution)/shard_map/jit(_where)/select_n | solution.py:27
  52.0 0.0 copy-done.2
  52.0 8.9 %convert_bitcast_fusion = bf16[64,128,512]{2,0,1:T(8,128)(2,1)} fusion(bf16[64,128,512]{2,0,1:T(8,128)(2,1)} %copy.25, bf16[64,64]{1,0:T(8,128)(2,1)S(1)} %copy-done.2), kind=kOutput, calls=%fused_computation.4 | convolution fusion | flops 541065216 | bytes 16785408 | tf_op jit(solution)/shard_map/pq,qmn->pmn/dot_general | solution.py:28
  60.9 11.3 %copy.26 = bf16[64,128,512]{2,1,0:T(8,128)(2,1)} copy(bf16[64,128,512]{2,0,1:T(8,128)(2,1)} %convert_bitcast_fusion) | data formatting | bytes 16777216 | tf_op jit(solution)/shard_map/convert_element_type | solution.py:28
  72.2 0.1 bitcast_select_fusion.1
  72.3 10.2 %convolution_convert_fusion = bf16[8192,512]{1,0:T(8,128)(2,1)} fusion(bf16[8192,512]{1,0:T(8,128)(2,1)} %bitcast.25, bf16[512,512]{0,1:T(8,128)(2,1)S(1)} %bitcast_select_fusion.1), kind=kOutput, calls=%fused_computation.3 | convolution fusion | flops 4299161600 | bytes 17301504 | tf_op jit(solution)/shard_map/dot_general | solution.py:15
  82.5 12.5 %reshape.138 = bf16[64,128,4,128]{3,2,1,0:T(4,128)(2,1)} reshape(bf16[8192,512]{1,0:T(8,128)(2,1)} %convolution_convert_fusion) | data formatting | bytes 16777216 | tf_op jit(solution)/shard_map/reshape | solution.py:36
  95.0 13.6 %copy.29 = bf16[64,128,4,128]{1,3,0,2:T(8,128)(2,1)} copy(bf16[64,128,4,128]{3,2,1,0:T(4,128)(2,1)} %reshape.138) | data formatting | bytes 16777216 | tf_op jit(solution)/shard_map/reshape | solution.py:36
  108.7 100.6 %all_to_all.4 = bf16[4,128,8192]{1,2,0:T(8,128)(2,1)} all-to-all(bf16[4,128,8192]{1,2,0:T(8,128)(2,1)} %bitcast.24), channel_id=1, replica_groups=mesh['blk'=8,'lay'=4] {'lay'}, dimensions={0} | all-to-all | bytes 16777216 | tf_op jit(solution)/shard_map/all_to_all | solution.py:40
  209.2 12.0 %copy.30 = bf16[4,128,8192]{2,1,0:T(8,128)(2,1)} copy(bf16[4,128,8192]{1,2,0:T(8,128)(2,1)} %all_to_all.4) | data formatting | bytes 16777216 | tf_op jit(solution)/shard_map/all_to_all | solution.py:40
  221.2 0.0 copy-start.1
  221.2 11.3 %fusion.6 = f32[512,512]{1,0:T(8,128)} fusion(bf16[512,8192]{1,0:T(8,128)(2,1)} %bitcast.27, bf16[8192,512]{1,0:T(8,128)(2,1)} %bitcast.26), kind=kOutput, calls=%fused_computation.38 | convolution fusion | flops 4294967296 | bytes 17825792 | tf_op jit(solution)/shard_map/dot_general | solution.py:42
  232.5 0.0 reduce-scatter.2.cloned.1.call-update
  232.5 0.0 all-reduce.2.cloned.1.call-start
  232.6 25.2 %reduce-scatter.2.cloned.1.call-done = f32[128,512]{1,0:T(8,128)} async-done(((f32[512,512]{1,0:T(8,128)}), f32[128,512]{1,0:T(8,128)}) %reduce-scatter.2.cloned.1.call-update) | async-done | bytes 262160 | tf_op jit(solution)/shard_map/reduce_scatter | solution.py:45
  257.7 0.0 all-reduce.2.cloned.1.call-update
  257.8 74.4 %all-reduce.2.cloned.1.call-done = f32[128,512]{1,0:T(8,128)} async-done(((f32[128,512]{1,0:T(8,128)}), f32[128,512]{1,0:T(8,128)}) %all-reduce.2.cloned.1.call-update) | async-done | bytes 262160 | tf_op jit(solution)/shard_map/psum | solution.py:46
  332.1 1.7 copy.32
  333.8 0.0 copy-done.1
  (7 shorter events, 0.1 us)
Async XLA Ops:
  6.5 11.6 %copy-start = (s32[64,16,16]{0,2,1:T(8,128)S(1)}, s32[64,16,16]{0,2,1:T(8,128)}, u32[]{:S(2)}) copy-start(s32[64,16,16]{0,2,1:T(8,128)} %param.7) | copy-start | bytes 196612
  6.5 251.2 %reduce-scatter.2.cloned.1.call-start = ((), (), s32[]{:S(2)}) async-start(), calls=%async_computation.2 | async-start | bytes 1310720 | tf_op jit(solution)/shard_map/reduce_scatter | solution.py:45
  39.4 12.6 %copy-start.2 = (bf16[64,64]{1,0:T(8,128)(2,1)S(1)}, bf16[64,64]{1,0:T(8,128)(2,1)}, u32[]{:S(2)}) copy-start(bf16[64,64]{1,0:T(8,128)(2,1)} %param.6) | copy-start | bytes 24580
  221.2 112.6 %copy-start.1 = (s32[64,16,16]{0,2,1:T(8,128)S(1)}, s32[64,16,16]{0,2,1:T(8,128)}, u32[]{:S(2)}) copy-start(s32[64,16,16]{0,2,1:T(8,128)} %param.7) | copy-start | bytes 196612
  232.5 99.6 %all-reduce.2.cloned.1.call-start = ((), (), s32[]{:S(2)}) async-start(), calls=%async_computation.3 | async-start | bytes 524288 | tf_op jit(solution)/shard_map/psum | solution.py:46
Sparse Core Ops, SparseCore 0:
  232.6 25.0 reduce-scatter.1
  261.1 70.9 all-reduce.1
where the time goes:
time: 343 us; the launch traced here: 341 us
  blocking collectives  109 us (32%)
  waiting for transfers between devices  99.6 us (29%)
  local copies, waits for them, and re-layouts  80 us (23%)
  matrix products  30.4 us (9%)
  between operations  13.5 us (4%)
  other arithmetic  7.89 us (2%)
    all_to_all x1, blocking collectives, per_device(): lax.all_to_all(outgoing, 'lay', split_axis=0, concat_axis=1, tiled=True)  101 us
    psum x1, waiting for transfers between devices, per_device(): return lax.psum(row_sums, 'blk')  74.4 us
    reshape x2, local copies, waits for them, and re-layouts, per_device(): inter.astype(jnp.bfloat16)  26.2 us
    reduce_scatter x1, waiting for transfers between devices, per_device(): lax.psum_scatter(partial_value, 'lay', scatter_dimension=0, tiled=True)  25.2 us
    unnamed x9, local copies, waits for them, and re-layouts  14.6 us
    select_n x1, local copies, waits for them, and re-layouts, per_device(): jnp.where(tile_mask > 0, three_centre, jnp.zeros_like(three_centre))  12.6 us
    all_to_all x1, local copies, waits for them, and re-layouts, per_device(): lax.all_to_all(outgoing, 'lay', split_axis=0, concat_axis=1, tiled=True)  12 us
    convert_element_type x1, local copies, waits for them, and re-layouts, per_device(): jnp.einsum('pq,qmn->pmn', metric, masked, preferred_element_type=jnp.floa...  11.3 us
  transfers between devices with their start and end apart: 2, of which 2 were waited for; matrix products, arithmetic and copies ran while one was open for 0% of the time, Pallas kernels for 0%

commit v1 on v0

--- a/solution.py
+++ b/solution.py
@@ -43,7 +43,8 @@
         moved, coeffs.reshape(group_size * row_count, ao_width), preferred_element_type=jnp.float32
     )
     row_sums = lax.psum_scatter(partial_value, "lay", scatter_dimension=0, tiled=True)
-    return lax.psum(row_sums, "blk")
+    _get_group = lambda inp, link_axis: jnp.sum(lax.all_gather(inp, axis_name=link_axis), 0)
+    return _get_group(row_sums, "blk")
 
 
 def solution(mesh):

time: 343 us -> 320 us (0.933)
  waiting for transfers between devices: 99.6 us -> 76.4 us
    psum x1 -> x0, waiting for transfers between devices: 74.4 us -> none  [per_device(): return lax.psum(row_sums, 'blk')]
    all_gather x0 -> x1, waiting for transfers between devices: none -> 51.2 us  [per_device(): lax.all_gather(inp, axis_name=link_axis)]
    unnamed x9 -> x8, local copies, waits for them, and re-layouts: 14.6 us -> 13 us
where the time goes in v1:
time: 320 us; the launch traced here: 318 us
  blocking collectives  109 us (34%)
  local copies, waits for them, and re-layouts  78.3 us (24%)
  waiting for transfers between devices  76.4 us (24%)
  matrix products  30.4 us (10%)
  between operations  13.5 us (4%)
  other arithmetic  10.4 us (3%)
    all_to_all x1, blocking collectives, per_device(): lax.all_to_all(outgoing, 'lay', split_axis=0, concat_axis=1, tiled=True)  101 us
    all_gather x1, waiting for transfers between devices, per_device(): lax.all_gather(inp, axis_name=link_axis)  51.2 us
    reshape x2, local copies, waits for them, and re-layouts, per_device(): inter.astype(jnp.bfloat16)  26.2 us
    reduce_scatter x1, waiting for transfers between devices, per_device(): lax.psum_scatter(partial_value, 'lay', scatter_dimension=0, tiled=True)  25.2 us
    unnamed x8, local copies, waits for them, and re-layouts  13 us
    select_n x1, local copies, waits for them, and re-layouts, per_device(): jnp.where(tile_mask > 0, three_centre, jnp.zeros_like(three_centre))  12.6 us
    all_to_all x1, local copies, waits for them, and re-layouts, per_device(): lax.all_to_all(outgoing, 'lay', split_axis=0, concat_axis=1, tiled=True)  12 us
    convert_element_type x1, local copies, waits for them, and re-layouts, per_device(): jnp.einsum('pq,qmn->pmn', metric, masked, preferred_element_type=jnp.floa...  11.3 us
  transfers between devices with their start and end apart: 2, of which 2 were waited for; matrix products, arithmetic and copies ran while one was open for 0% of the time, Pallas kernels for 0%

profile of v1, /device:TPU:0, one launch (start us, length us, event | category | flops | bytes accessed | tf_op | source)
XLA Modules:
  0.0 318.3 jit_solution(17004688668480662849)
XLA Ops:
  6.5 0.0 copy-start
  6.5 0.0 reduce-scatter.2.cloned.1.call-start
  6.6 1.0 copy.28
  7.7 1.7 gather_fusion.1
  9.4 0.1 copy.27
  9.5 8.7 %all_gather.9 = bf16[512,512]{0,1:T(8,128)(2,1)S(1)} all-gather(bf16[128,512]{0,1:T(8,128)(2,1)S(1)} %copy.28), channel_id=1, replica_groups=mesh['blk'=8,'lay'=4] {'lay'}, dimensions={0}, use_global_device_ids=true | all-gather | bytes 655360 | tf_op jit(solution)/shard_map/all_gather | solution.py:33
  18.2 0.0 copy-done
  18.2 0.8 gather_fusion
  18.9 0.3 fusion
  19.2 0.7 copy.23
  19.9 11.9 %copy.24 = bf16[64,128,512]{1,2,0:T(8,128)(2,1)} copy(bf16[64,128,512]{2,1,0:T(8,128)(2,1)} %param.5) | data formatting | bytes 16777216 | tf_op args[0]
  31.9 7.5 %bitcast_select_fusion = bf16[64,128,512]{1,2,0:T(8,128)(2,1)} fusion(bf16[64,128,512]{1,2,0:T(8,128)(2,1)} %copy.24, pred[64,128,16]{1,2,0:T(8,128)(4,1)S(1)} %copy.23), kind=kLoop, calls=%fused_computation.2 | loop fusion | flops 4194304 | bytes 16908288 | tf_op jit(solution)/shard_map/jit(_where)/select_n | solution.py:27
  39.4 0.0 copy-start.2
  39.4 12.6 %copy.25 = bf16[64,128,512]{2,0,1:T(8,128)(2,1)} copy(bf16[64,128,512]{1,2,0:T(8,128)(2,1)} %bitcast_select_fusion) | data formatting | bytes 16777216 | tf_op jit(solution)/shard_map/jit(_where)/select_n | solution.py:27
  52.0 0.0 copy-done.2
  52.0 8.9 %convert_bitcast_fusion = bf16[64,128,512]{2,0,1:T(8,128)(2,1)} fusion(bf16[64,128,512]{2,0,1:T(8,128)(2,1)} %copy.25, bf16[64,64]{1,0:T(8,128)(2,1)S(1)} %copy-done.2), kind=kOutput, calls=%fused_computation.4 | convolution fusion | flops 541065216 | bytes 16785408 | tf_op jit(solution)/shard_map/pq,qmn->pmn/dot_general | solution.py:28
  60.9 11.3 %copy.26 = bf16[64,128,512]{2,1,0:T(8,128)(2,1)} copy(bf16[64,128,512]{2,0,1:T(8,128)(2,1)} %convert_bitcast_fusion) | data formatting | bytes 16777216 | tf_op jit(solution)/shard_map/convert_element_type | solution.py:28
  72.2 0.1 bitcast_select_fusion.1
  72.3 10.2 %convolution_convert_fusion = bf16[8192,512]{1,0:T(8,128)(2,1)} fusion(bf16[8192,512]{1,0:T(8,128)(2,1)} %bitcast.26, bf16[512,512]{0,1:T(8,128)(2,1)S(1)} %bitcast_select_fusion.1), kind=kOutput, calls=%fused_computation.3 | convolution fusion | flops 4299161600 | bytes 17301504 | tf_op jit(solution)/shard_map/dot_general | solution.py:15
  82.5 12.5 %reshape.138 = bf16[64,128,4,128]{3,2,1,0:T(4,128)(2,1)} reshape(bf16[8192,512]{1,0:T(8,128)(2,1)} %convolution_convert_fusion) | data formatting | bytes 16777216 | tf_op jit(solution)/shard_map/reshape | solution.py:36
  95.0 13.6 %copy.29 = bf16[64,128,4,128]{1,3,0,2:T(8,128)(2,1)} copy(bf16[64,128,4,128]{3,2,1,0:T(4,128)(2,1)} %reshape.138) | data formatting | bytes 16777216 | tf_op jit(solution)/shard_map/reshape | solution.py:36
  108.7 100.6 %all_to_all.4 = bf16[4,128,8192]{1,2,0:T(8,128)(2,1)} all-to-all(bf16[4,128,8192]{1,2,0:T(8,128)(2,1)} %bitcast.25), channel_id=1, replica_groups=mesh['blk'=8,'lay'=4] {'lay'}, dimensions={0} | all-to-all | bytes 16777216 | tf_op jit(solution)/shard_map/all_to_all | solution.py:40
  209.2 12.0 %copy.30 = bf16[4,128,8192]{2,1,0:T(8,128)(2,1)} copy(bf16[4,128,8192]{1,2,0:T(8,128)(2,1)} %all_to_all.4) | data formatting | bytes 16777216 | tf_op jit(solution)/shard_map/all_to_all | solution.py:40
  221.2 0.0 copy-start.1
  221.2 11.3 %fusion.6 = f32[512,512]{1,0:T(8,128)} fusion(bf16[512,8192]{1,0:T(8,128)(2,1)} %bitcast.28, bf16[8192,512]{1,0:T(8,128)(2,1)} %bitcast.27), kind=kOutput, calls=%fused_computation.38 | convolution fusion | flops 4294967296 | bytes 17825792 | tf_op jit(solution)/shard_map/dot_general | solution.py:42
  232.5 0.0 reduce-scatter.2.cloned.1.call-update
  232.5 0.0 all-gather.3.cloned.1.call-start
  232.6 25.2 %reduce-scatter.2.cloned.1.call-done = f32[128,512]{1,0:T(8,128)} async-done(((f32[512,512]{1,0:T(8,128)}), f32[128,512]{1,0:T(8,128)}) %reduce-scatter.2.cloned.1.call-update) | async-done | bytes 262160 | tf_op jit(solution)/shard_map/reduce_scatter | solution.py:45
  257.7 0.0 all-gather.3.cloned.1.call-update
  257.8 51.2 %all-gather.3.cloned.1.call-done = f32[1024,512]{1,0:T(8,128)} async-done(((f32[128,512]{1,0:T(8,128)}), f32[1024,512]{1,0:T(8,128)}) %all-gather.3.cloned.1.call-update) | async-done | bytes 2097168 | tf_op jit(solution)/shard_map/all_gather | solution.py:46
  309.0 2.5 reduce_sum.9
  311.5 0.0 copy-done.1
  (7 shorter events, 0.1 us)
Async XLA Ops:
  6.5 11.6 %copy-start = (s32[64,16,16]{0,2,1:T(8,128)S(1)}, s32[64,16,16]{0,2,1:T(8,128)}, u32[]{:S(2)}) copy-start(s32[64,16,16]{0,2,1:T(8,128)} %param.7) | copy-start | bytes 196612
  6.5 251.2 %reduce-scatter.2.cloned.1.call-start = ((), (), s32[]{:S(2)}) async-start(), calls=%async_computation.2 | async-start | bytes 1310720 | tf_op jit(solution)/shard_map/reduce_scatter | solution.py:45
  39.4 12.6 %copy-start.2 = (bf16[64,64]{1,0:T(8,128)(2,1)S(1)}, bf16[64,64]{1,0:T(8,128)(2,1)}, u32[]{:S(2)}) copy-start(bf16[64,64]{1,0:T(8,128)(2,1)} %param.6) | copy-start | bytes 24580
  221.2 90.3 %copy-start.1 = (s32[64,16,16]{0,2,1:T(8,128)S(1)}, s32[64,16,16]{0,2,1:T(8,128)}, u32[]{:S(2)}) copy-start(s32[64,16,16]{0,2,1:T(8,128)} %param.7) | copy-start | bytes 196612
  232.5 76.5 %all-gather.3.cloned.1.call-start = ((), (), s32[]{:S(2)}) async-start(), calls=%async_computation.3 | async-start | bytes 2359296 | tf_op jit(solution)/shard_map/all_gather | solution.py:46
Sparse Core Ops, SparseCore 0:
  232.6 25.0 reduce-scatter.1
  259.9 49.0 all-gather.2
